TPU v7x, 32 devices: a whole 2x2x4 slice. The times are simulated.
32 devices in a mesh: ep: 4 (over y, x), fsdp: 8 (over z, core).
Axes of the slice: x: 2, y: 2, z: 4, core: 2. Of those that a mesh axis runs over, the one named last changes fastest.
Arguments:
- train_gate: float32 [128, 2048, 768], P('ep', 'fsdp'), may hold values from -0.1875 to 0.1875
- other_gate: bfloat16 [128, 2048, 768], P('ep', 'fsdp'), may hold values from -0.0625 to 0.0625
- train_up: float32 [128, 2048, 768], P('ep', 'fsdp'), may hold values from -0.1875 to 0.1875
- other_up: bfloat16 [128, 2048, 768], P('ep', 'fsdp'), may hold values from -0.0625 to 0.0625
- router_weight: float32 [2048, 128], P('fsdp', 'ep'), may hold values from -0.125 to 0.125
- router_gain: float32 [2048], P('fsdp'), may hold values from 0.25 to 1.75
Outputs:
- ready_gate: bfloat16 [128, 2048, 768], P(('ep', 'fsdp'))
- ready_up: bfloat16 [128, 2048, 768], P(('ep', 'fsdp'))
- scale_gate: float32 [128, 768], P(('ep', 'fsdp'))
- scale_up: float32 [128, 768], P(('ep', 'fsdp'))
- serve_router: bfloat16 [2048, 128], replicated
All inputs are finite; a program needn't handle non-finite values. Where the computation divides by a largest or mean magnitude, that divisor is 1e-20 or more.
Results may differ from a plain program's by a relative error of at most 0.013.
Values may be sent and summed in bfloat16 or wider, within the bound.
A program may use at most 192 MiB of HBM per device.

v0:
```python
import jax
import jax.numpy as jnp
from jax import lax
from jax.sharding import PartitionSpec as P

D_MODEL = 2048


def shards(train_gate, other_gate, train_up, other_up, router_weight, router_gain):
    latest_gate = train_gate + other_gate.astype(jnp.float32)
    latest_up = train_up + other_up.astype(jnp.float32)
    total_gate, total_up = (
        lax.psum(jnp.sum(jnp.abs(latest_gate), axis=1).astype(jnp.bfloat16), "fsdp").astype(
            jnp.float32
        ),
        lax.psum(jnp.sum(jnp.abs(latest_up), axis=1).astype(jnp.bfloat16), "fsdp").astype(
            jnp.float32
        ),
    )
    scale_gate = total_gate / D_MODEL
    scale_up = total_up / D_MODEL
    narrow_gate, narrow_up = (
        (latest_gate / jnp.expand_dims(scale_gate, 1)).astype(jnp.bfloat16),
        (latest_up / jnp.expand_dims(scale_up, 1)).astype(jnp.bfloat16),
    )
    ready_gate, ready_up = (
        lax.all_to_all(narrow_gate, "fsdp", split_axis=0, concat_axis=1, tiled=True),
        lax.all_to_all(narrow_up, "fsdp", split_axis=0, concat_axis=1, tiled=True),
    )
    scale_gate = lax.dynamic_slice_in_dim(
        scale_gate, lax.axis_index("fsdp") * ready_gate.shape[0], ready_gate.shape[0], axis=0
    )
    scale_up = lax.dynamic_slice_in_dim(
        scale_up, lax.axis_index("fsdp") * ready_up.shape[0], ready_up.shape[0], axis=0
    )
    part_router = (router_weight * router_gain[:, None]).astype(jnp.bfloat16)
    row_router = lax.all_gather(part_router, "fsdp", axis=0, tiled=True)
    serve_router = lax.all_gather(row_router, "ep", axis=1, tiled=True)
    return (ready_gate, ready_up, scale_gate, scale_up, serve_router)


def solution(mesh):
    placed = (
        P("ep", "fsdp", None),
        P("ep", "fsdp", None),
        P("ep", "fsdp", None),
        P("ep", "fsdp", None),
        P("fsdp", "ep"),
        P("fsdp"),
    )
    return jax.shard_map(
        shards,
        mesh=mesh,
        in_specs=placed,
        out_specs=(
            P(("ep", "fsdp"), None, None),
            P(("ep", "fsdp"), None, None),
            P(("ep", "fsdp"), None),
            P(("ep", "fsdp"), None),
            P(),
        ),
        check_vma=False,
    )
```

profile of v0, /device:TPU:1, one launch (start us, length us, event | category | flops | bytes accessed | tf_op | source)
XLA Modules:
  0.0 709.6 jit_solution(16841271009129784802)
XLA Ops:
  7.2 0.0 all-reduce.3.cloned.1.call-start
  7.2 25.2 %abs_reduce_fusion = (bf16[32,768]{1,0:T(8,128)(2,1)}, bf16[32,768]{1,0:T(8,128)(2,1)}) fusion(f32[32,256,768]{2,1,0:T(8,128)} %param.8, bf16[32,256,768]{2,1,0:T(8,128)(2,1)} %param.9, f32[32,256,768]{2,1,0:T(8,128)} %param.6, bf16[32,256,768]{2,1,0:T(8,128)(2,1)} %param.7), kind=kLoop, calls=%fused_computation.1 | loop fusion | flops 50282496 | bytes 75595776 | tf_op jit(solution)/shard_map/reduce_sum | solution.py:16
  32.4 0.0 all-reduce.3.cloned.1.call-update
  32.4 54.1 %all-reduce.3.cloned.1.call-done = (bf16[32,768]{1,0:T(8,128)(2,1)}, bf16[32,768]{1,0:T(8,128)(2,1)}) async-done(((bf16[32,768]{1,0:T(8,128)(2,1)}, bf16[32,768]{1,0:T(8,128)(2,1)}), (bf16[32,768]{1,0:T(8,128)(2,1)}, bf16[32,768]{1,0:T(8,128)(2,1)})) %all-reduce.3.cloned.1.call-update) | async-done | bytes 98320 | tf_op jit(solution)/shard_map/psum | solution.py:13
  86.5 0.8 convert_multiply_fusion.1
  87.3 17.2 %divide_convert_fusion.1 = bf16[32,256,768]{2,1,0:T(8,128)(2,1)} fusion(f32[32,256,768]{2,1,0:T(8,128)} %param.6, bf16[32,256,768]{2,1,0:T(8,128)(2,1)} %param.7, f32[32,768]{1,0:T(8,128)S(1)} %convert_multiply_fusion.1), kind=kLoop, calls=%fused_computation.3 | loop fusion | flops 25165824 | bytes 50429952 | tf_op jit(solution)/shard_map/convert_element_type | solution.py:23
  104.5 0.0 copy-start
  104.5 6.8 all-to-all-start
  111.3 0.0 copy-done
  111.3 17.4 %divide_convert_fusion = bf16[32,256,768]{2,1,0:T(8,128)(2,1)} fusion(f32[32,256,768]{2,1,0:T(8,128)} %param.8, bf16[32,256,768]{2,1,0:T(8,128)(2,1)} %param.9, f32[32,768]{1,0:T(8,128)S(1)} %convert_multiply_fusion), kind=kLoop, calls=%fused_computation | loop fusion | flops 25165824 | bytes 50429952 | tf_op jit(solution)/shard_map/convert_element_type | solution.py:24
  128.7 0.0 copy-start.1
  128.7 0.0 copy-start.2
  128.7 255.1 %all-to-all-done = bf16[32,256,768]{2,1,0:T(8,128)(2,1)} async-done(((bf16[32,256,768]{2,1,0:T(8,128)(2,1)}), bf16[32,256,768]{2,1,0:T(8,128)(2,1)}, u32[]{:S(2)}, u32[]{:S(2)}) %all-to-all-start) | async-done | bytes 12582944 | tf_op jit(solution)/shard_map/all_to_all | solution.py:27
  383.8 6.7 all-to-all-start.1
  390.4 0.0 copy-done.1
  390.4 0.0 copy-done.2
  390.4 279.9 %all_gather.6 = bf16[2048,32]{0,1:T(8,128)(2,1)S(1)} all-gather(bf16[256,32]{0,1:T(8,128)(2,1)S(1)} %multiply_convert_fusion), channel_id=1, replica_groups=mesh['ep'=4,'fsdp'=8] {'fsdp'}, dimensions={0}, use_global_device_ids=true | all-gather | bytes 147456 | tf_op jit(solution)/shard_map/all_gather | solution.py:37
  670.4 8.8 %all_gather.7 = bf16[2048,128]{0,1:T(8,128)(2,1)S(1)} all-gather(bf16[2048,32]{0,1:T(8,128)(2,1)S(1)} %all_gather.6), channel_id=1, replica_groups=mesh['ep'=4,'fsdp'=8] {'ep'}, dimensions={1}, use_global_device_ids=true | all-gather | bytes 655360 | tf_op jit(solution)/shard_map/all_gather | solution.py:38
  679.2 1.0 copy.16
  680.2 0.6 constant_dynamic-slice_fusion
  680.8 0.6 constant_dynamic-slice_fusion.1
  681.4 10.7 %copy.14 = bf16[8,4,256,768]{3,2,0,1:T(8,128)(2,1)} copy(bf16[8,4,256,768]{3,2,1,0:T(8,128)(2,1)} %bitcast) | data formatting | bytes 25165824 | tf_op jit(solution)/shard_map/all_to_all | solution.py:27
  692.1 0.0 all-to-all-done.1
  692.1 10.7 %copy.15 = bf16[8,4,256,768]{3,2,0,1:T(8,128)(2,1)} copy(bf16[8,4,256,768]{3,2,1,0:T(8,128)(2,1)} %bitcast.3) | data formatting | bytes 25165824 | tf_op jit(solution)/shard_map/all_to_all | solution.py:28
  (2 shorter events, 0.0 us)
Async XLA Ops:
  7.2 79.3 %all-reduce.3.cloned.1.call-start = ((), (), s32[]{:S(2)}) async-start(), calls=%async_computation.2 | async-start | bytes 196608 | tf_op jit(solution)/shard_map/psum | solution.py:13
  104.5 6.8 copy-start
  104.5 279.2 %all-to-all-start = ((bf16[32,256,768]{2,1,0:T(8,128)(2,1)}), bf16[32,256,768]{2,1,0:T(8,128)(2,1)}, u32[]{:S(2)}, u32[]{:S(2)}) async-start(bf16[32,256,768]{2,1,0:T(8,128)(2,1)} %divide_convert_fusion.1), calls=%async_computation | async-start | bytes 25165824 | tf_op jit(solution)/shard_map/all_to_all | solution.py:27
  128.7 261.7 %copy-start.1 = (f32[256,32]{0,1:T(8,128)S(1)}, f32[256,32]{0,1:T(8,128)}, u32[]{:S(2)}) copy-start(f32[256,32]{0,1:T(8,128)} %param.10) | copy-start | bytes 98308
  128.7 261.7 %copy-start.2 = (f32[256]{0:T(256)S(1)}, f32[256]{0:T(256)}, u32[]{:S(2)}) copy-start(f32[256]{0:T(256)} %param.11) | copy-start | bytes 3076
  383.8 308.3 %all-to-all-start.1 = ((bf16[32,256,768]{2,1,0:T(8,128)(2,1)}), bf16[32,256,768]{2,1,0:T(8,128)(2,1)}, u32[]{:S(2)}, u32[]{:S(2)}) async-start(bf16[32,256,768]{2,1,0:T(8,128)(2,1)} %divide_convert_fusion), calls=%async_computation.1 | async-start | bytes 25165824 | tf_op jit(solution)/shard_map/all_to_all | solution.py:28
Sparse Core Ops, SparseCore 0:
  32.5 53.9 all-reduce.2
where the time goes:
time: 712 us; the launch traced here: 710 us
  waiting for transfers between devices  309 us (43%)
  blocking collectives  289 us (41%)
  other arithmetic  60.6 us (9%)
  local copies, waits for them, and re-layouts  23.6 us (3%)
  between operations  14.1 us (2%)
  starting transfers between devices  13.4 us (2%)
    all_gather x1, blocking collectives, shards(): row_router = lax.all_gather(part_router, 'fsdp', axis=0, tiled=True)  280 us
    all_to_all x1, waiting for transfers between devices, shards(): lax.all_to_all(narrow_gate, 'fsdp', split_axis=0, concat_axis=1, tiled=True)  255 us
    psum x1, waiting for transfers between devices, shards(): lax.psum(jnp.sum(jnp.abs(latest_gate), axis=1).astype(jnp.bfloat16), 'fsdp')  54.1 us
    reduce_sum x1, other arithmetic, shards(): jnp.sum(jnp.abs(latest_up), axis=1).astype(jnp.bfloat16)  25.2 us
    convert_element_type x1, other arithmetic, shards(): (latest_up / jnp.expand_dims(scale_up, 1)).astype(jnp.bfloat16)  17.4 us
    convert_element_type x1, other arithmetic, shards(): (latest_gate / jnp.expand_dims(scale_gate, 1)).astype(jnp.bfloat16)  17.2 us
  transfers between devices with their start and end apart: 3, of which 2 were waited for; matrix products, arithmetic and copies ran while one was open for 4% of the time, Pallas kernels for 0%

commit v1 on v0

v1 whole, which is shorter than its diff:
```python
import functools

import jax
import jax.numpy as jnp
from jax import lax
from jax.experimental import pallas as pl
from jax.experimental.pallas import tpu as pltpu
from jax.sharding import PartitionSpec as P

MESH = pl.DeviceIdType.MESH
SLOTS = 4
ROWS = 32


def exchange(
    n,
    groups,
    train_gate,
    other_gate,
    train_up,
    other_up,
    router,
    out_gate,
    out_up,
    out_router,
    wide,
    narrow,
    send,
    wide_sem,
    narrow_sem,
    send_sem,
    gate_sem,
    up_sem,
    row_send,
    row_recv,
    col_send,
    col_recv,
):
    me = lax.axis_index("fsdp")
    ep = lax.axis_index("ep")
    experts, rows, _ = train_gate.shape
    own = experts // n
    band = router.shape[0]

    barrier = pltpu.get_barrier_semaphore()
    for k in range(1, n):
        pl.semaphore_signal(
            barrier, inc=1, device_id={"fsdp": lax.rem(me + k, n)}, device_id_type=MESH
        )
    for k in range(1, groups):
        pl.semaphore_signal(
            barrier, inc=1, device_id={"ep": lax.rem(ep + k, groups)}, device_id_type=MESH
        )

    chips = n // 2
    chip, core = me // 2, lax.rem(me, 2)
    per = 4 * own
    near = jnp.minimum(chip, chips - 1 - chip)
    forward = jnp.where(chip < chips - near - 1, 1, -1)
    both = 2 * near * per
    far = (chips - 1) * per

    def piece_of(t):
        pair = lax.rem(t, 2 * per)
        tail = t - both
        two = t < both
        away = t < far
        shift = jnp.where(
            two,
            (t // (2 * per) + 1) * (1 - 2 * lax.rem(pair, 2)),
            (near + 1 + tail // per) * forward,
        )
        piece = jnp.where(two, pair // 2, lax.rem(tail, per))
        piece = jnp.where(away, piece, t - far)
        to_chip = jnp.where(away, chip + shift, chip)
        which = lax.rem(piece, 2)
        rest = piece // 2
        on_core = jnp.where(away, which, jnp.where(piece < 2 * own, 1 - core, core))
        rest = jnp.where(away, rest, lax.rem(piece, 2 * own))
        return to_chip * 2 + on_core, rest // 2, lax.rem(rest, 2)

    steps = 2 * experts
    remote = steps - 2 * own

    def load(t, act):
        device, expert, tensor = piece_of(t)
        slot = lax.rem(t, SLOTS)
        at = device * own + expert
        for k, (a, b) in enumerate(((train_gate, other_gate), (train_up, other_up))):

            @pl.when(tensor == k)
            def _():
                for source, target, sem in ((a, wide, wide_sem), (b, narrow, narrow_sem)):
                    copy = pltpu.make_async_copy(source.at[at], target.at[slot], sem.at[slot])
                    getattr(copy, act)()

    def ship(t):
        device, expert, tensor = piece_of(t)
        for k, (out, sem) in enumerate(((out_gate, gate_sem), (out_up, up_sem))):
            place = out.at[expert, pl.ds(me * rows, rows), :]

            @pl.when((tensor == k) & (t < remote))
            def _():
                pltpu.make_async_remote_copy(
                    src_ref=send.at[t],
                    dst_ref=place,
                    send_sem=send_sem,
                    recv_sem=sem,
                    device_id={"fsdp": device},
                    device_id_type=MESH,
                ).start()

            @pl.when((tensor == k) & (t >= remote))
            def _():
                pltpu.make_async_copy(send.at[t], place, sem).start()

    for t in range(SLOTS - 1):
        load(t, "start")
    pl.semaphore_wait(barrier, n - 1 + groups - 1)

    home = out_router.at[me, pl.ds(ep * band, band), :]
    pltpu.make_async_copy(router, home, row_recv).start()
    for k in range(1, n):
        pltpu.make_async_remote_copy(
            src_ref=router,
            dst_ref=home,
            send_sem=row_send,
            recv_sem=row_recv,
            device_id={"fsdp": lax.rem(me + k, n)},
            device_id_type=MESH,
        ).start()

    def step(t, _):
        slot = lax.rem(t, SLOTS)

        @pl.when(t + SLOTS - 1 < steps)
        def _():
            load(t + SLOTS - 1, "start")

        load(t, "wait")

        def chunk(r, _):
            at = pl.ds(pl.multiple_of(r * ROWS, ROWS), ROWS)
            latest = wide[slot, at, :] + narrow[slot, at, :].astype(jnp.float32)
            send[t, at, :] = latest.astype(jnp.bfloat16)
            return 0

        lax.fori_loop(0, rows // ROWS, chunk, 0)

        @pl.when(t > 0)
        def _():
            ship(t - 1)

        return 0

    lax.fori_loop(0, steps, step, 0)
    ship(steps - 1)

    columns = out_router.at[:, pl.ds(ep * band, band), :]
    pltpu.make_async_copy(columns, columns, row_recv).wait()
    for k in range(1, groups):
        pltpu.make_async_remote_copy(
            src_ref=columns,
            dst_ref=columns,
            send_sem=col_send,
            recv_sem=col_recv,
            device_id={"ep": lax.rem(ep + k, groups)},
            device_id_type=MESH,
        ).start()
    others = out_router.at[:, pl.ds(0, (groups - 1) * band), :]
    pltpu.make_async_copy(others, others, col_recv).wait()
    pltpu.make_async_copy(others, others, col_send).wait()
    sent = out_router.at[pl.ds(0, n - 1), pl.ds(0, band), :]
    pltpu.make_async_copy(sent, sent, row_send).wait()

    gone = send.at[pl.ds(0, remote)]
    pltpu.make_async_copy(gone, gone, send_sem).wait()
    pltpu.make_async_copy(out_gate, out_gate, gate_sem).wait()
    pltpu.make_async_copy(out_up, out_up, up_sem).wait()


def finish(raw_gate, raw_up, ready_gate, ready_up, scale_gate, scale_up):
    depth, wide = raw_gate.shape[1], raw_gate.shape[2]
    part = 32
    for raw, ready, scale in ((raw_gate, ready_gate, scale_gate), (raw_up, ready_up, scale_up)):

        def add(r, total):
            at = pl.ds(pl.multiple_of(r * part, part), part)
            size = jnp.abs(raw[0, at, :].astype(jnp.float32))
            return total + jnp.sum(size.reshape(part // 8, 8, wide), axis=0)

        total = lax.fori_loop(0, depth // part, add, jnp.zeros((8, wide), jnp.float32))
        mean = jnp.sum(total, axis=0, keepdims=True) / depth
        scale[0] = mean
        over = 1.0 / mean

        def divide(r, _):
            at = pl.ds(pl.multiple_of(r * part, part), part)
            ready[0, at, :] = (raw[0, at, :].astype(jnp.float32) * over).astype(jnp.bfloat16)
            return 0

        lax.fori_loop(0, depth // part, divide, 0)


def shards(n, groups, train_gate, other_gate, train_up, other_up, router_weight, router_gain):
    experts, rows, width = train_gate.shape
    own = experts // n
    part_router = (router_weight * router_gain[:, None]).astype(jnp.bfloat16).T
    band, depth = part_router.shape
    anywhere = pl.BlockSpec(memory_space=pl.ANY)
    landed = jax.ShapeDtypeStruct((own, n * rows, width), jnp.bfloat16)
    raw_gate, raw_up, router = pl.pallas_call(
        functools.partial(exchange, n, groups),
        out_shape=(
            landed,
            landed,
            jax.ShapeDtypeStruct((n, groups * band, depth), jnp.bfloat16),
        ),
        in_specs=[anywhere] * 5,
        out_specs=(anywhere,) * 3,
        scratch_shapes=[
            pltpu.VMEM((SLOTS, rows, width), jnp.float32),
            pltpu.VMEM((SLOTS, rows, width), jnp.bfloat16),
            pltpu.VMEM((2 * experts, rows, width), jnp.bfloat16),
            pltpu.SemaphoreType.DMA((SLOTS,)),
            pltpu.SemaphoreType.DMA((SLOTS,)),
        ]
        + [pltpu.SemaphoreType.DMA] * 7,
        compiler_params=pltpu.CompilerParams(
            collective_id=0, has_side_effects=True, vmem_limit_bytes=56 * 2**20
        ),
    )(train_gate, other_gate, train_up, other_up, part_router)

    cols = 256
    block = pl.BlockSpec((1, n * rows, cols), lambda e, j: (e, 0, j))
    line = pl.BlockSpec((1, 1, cols), lambda e, j: (e, 0, j))
    ready_gate, ready_up, scale_gate, scale_up = pl.pallas_call(
        finish,
        grid=(own, width // cols),
        out_shape=(landed, landed) + (jax.ShapeDtypeStruct((own, 1, width), jnp.float32),) * 2,
        in_specs=[block, block],
        out_specs=(block, block, line, line),
        compiler_params=pltpu.CompilerParams(vmem_limit_bytes=40 * 2**20),
    )(raw_gate, raw_up)
    serve_router = router.transpose(0, 2, 1).reshape(n * depth, groups * band)
    return (
        ready_gate,
        ready_up,
        scale_gate.reshape(own, width),
        scale_up.reshape(own, width),
        serve_router,
    )


def solution(mesh):
    placed = (
        P("ep", "fsdp", None),
        P("ep", "fsdp", None),
        P("ep", "fsdp", None),
        P("ep", "fsdp", None),
        P("fsdp", "ep"),
        P("fsdp"),
    )
    return jax.shard_map(
        functools.partial(shards, mesh.shape["fsdp"], mesh.shape["ep"]),
        mesh=mesh,
        in_specs=placed,
        out_specs=(
            P(("ep", "fsdp"), None, None),
            P(("ep", "fsdp"), None, None),
            P(("ep", "fsdp"), None),
            P(("ep", "fsdp"), None),
            P(),
        ),
        check_vma=False,
    )
```

time: 712 us -> 586 us (0.82)
  Pallas kernels: 0 us -> 577 us
  waiting for transfers between devices: 309 us -> 0 us
  blocking collectives: 289 us -> 0 us
  other arithmetic: 60.6 us -> 1.37 us
  local copies, waits for them, and re-layouts: 23.6 us -> 6.18 us
  between operations: 14.1 us -> 0.65 us
  starting transfers between devices: 13.4 us -> 0 us
    pallas_call x0 -> x2, Pallas kernels: none -> 577 us  [the longest x1 549 us: shards(): pl.pallas_call(functools.partial(exchange, n, groups), out_shape=(landed,...]
    all_gather x2 -> x0, blocking collectives: 289 us -> none  [the longest x1 280 us: shards(): row_router = lax.all_gather(part_router, 'fsdp', axis=0, tiled=True)]
    all_to_all x2 -> x0, waiting for transfers between devices: 255 us -> none  [the longest x1 255 us: shards(): lax.all_to_all(narrow_gate, 'fsdp', split_axis=0, concat_axis=1, tiled=True)]
    psum x1 -> x0, waiting for transfers between devices: 54.1 us -> none  [shards(): lax.psum(jnp.sum(jnp.abs(latest_gate), axis=1).astype(jnp.bfloat16), 'fsdp')]
    convert_element_type x3 -> x0, other arithmetic: 34.6 us -> none  [the longest x1 17.4 us: shards(): (latest_up / jnp.expand_dims(scale_up, 1)).astype(jnp.bfloat16)]
    reduce_sum x1 -> x0, other arithmetic: 25.2 us -> none  [shards(): jnp.sum(jnp.abs(latest_up), axis=1).astype(jnp.bfloat16)]
    all_to_all x2 -> x0, local copies, waits for them, and re-layouts: 21.4 us -> none  [the longest x1 10.7 us: shards(): lax.all_to_all(narrow_up, 'fsdp', split_axis=0, concat_axis=1, tiled=True)]
    all_to_all x2 -> x0, starting transfers between devices: 13.4 us -> none  [the longest x1 6.75 us: shards(): lax.all_to_all(narrow_gate, 'fsdp', split_axis=0, concat_axis=1, tiled=True)]
  transfers between devices with their start and end apart: 3 -> 0, of which waited for: 2 -> 0; matrix products, arithmetic and copies ran while one was open for 4% -> 0% of each run, Pallas kernels for 0% -> 0%
where the time goes in v1:
time: 586 us; the launch traced here: 585 us
  Pallas kernels  577 us (98%)
  local copies, waits for them, and re-layouts  6.18 us (1%)
    pallas_call x1, Pallas kernels, shards(): pl.pallas_call(functools.partial(exchange, n, groups), out_shape=(landed,...  549 us
    pallas_call x1, Pallas kernels, shards(): pl.pallas_call(finish, grid=(own, width // cols), out_shape=(landed, land...  28.2 us

profile of v1, /device:TPU:1, one launch (start us, length us, event | category | flops | bytes accessed | tf_op | source)
XLA Modules:
  0.0 585.3 jit_solution(11580925179868928667)
XLA Ops:
  0.6 1.4 fusion.router
  2.0 548.9 %shard_map.101 = (bf16[4,2048,768]{2,1,0:T(8,128)(2,1)}, bf16[4,2048,768]{2,1,0:T(8,128)(2,1)}, bf16[8,128,256]{2,1,0:T(8,128)(2,1)}) custom-call(f32[32,256,768]{2,1,0:T(8,128)} %train_gate.1, bf16[32,256,768]{2,1,0:T(8,128)(2,1)} %other_gate.1, f32[32,256,768]{2,1,0:T(8,128)} %train_up.1, bf16[32,256,768]{2,1,0:T(8,128)(2,1)} %other_up.1, ...), custom_call_target="tpu_custom_call" | custom-call | tf_op jit(solution)/shard_map/pallas_call | solution.py:212
  550.9 0.0 copy-start
  550.9 4.6 copy-done
  555.5 0.0 copy-start.1
  555.5 28.2 %shard_map.102 = (bf16[4,2048,768]{2,1,0:T(8,128)(2,1)}, bf16[4,2048,768]{2,1,0:T(8,128)(2,1)}, f32[4,1,768]{2,1,0:T(1,128)S(1)}, f32[4,1,768]{2,1,0:T(1,128)S(1)}) custom-call(bf16[4,2048,768]{2,1,0:T(8,128)(2,1)S(1)} %copy-done, bf16[4,2048,768]{2,1,0:T(8,128)(2,1)} %get-tuple-element.13.raw_up), custom_call_target="tpu_custom_call" | custom-call | tf_op jit(solution)/shard_map/pallas_call | solution.py:237
  583.7 0.6 copy_bitcast_fusion
  584.3 0.0 copy-done.1
  584.3 1.0 copy.11
Async XLA Ops:
  550.9 4.6 copy-start
  555.5 28.8 %copy-start.1 = (bf16[8,128,256]{2,1,0:T(8,128)(2,1)S(1)}, bf16[8,128,256]{2,1,0:T(8,128)(2,1)}, u32[]{:S(2)}) copy-start(bf16[8,128,256]{2,1,0:T(8,128)(2,1)} %get-tuple-element.18) | copy-start | bytes 1572868

commit v2 on v1

v2 whole, which is shorter than its diff:
```python
import functools

import jax
import jax.numpy as jnp
from jax import lax
from jax.experimental import pallas as pl
from jax.experimental.pallas import tpu as pltpu
from jax.sharding import PartitionSpec as P

MESH = pl.DeviceIdType.MESH
SLOTS = 4
ROWS = 32


def exchange(
    n,
    groups,
    train_gate,
    other_gate,
    train_up,
    other_up,
    router,
    mean,
    landed,
    out_router,
    wide,
    narrow,
    send,
    total,
    wide_sem,
    narrow_sem,
    land_sem,
    send_sem,
    row_send,
    row_recv,
    col_send,
    col_recv,
):
    me = lax.axis_index("fsdp")
    ep = lax.axis_index("ep")
    experts, rows, width = train_gate.shape
    own = experts // n
    band = router.shape[0]

    barrier = pltpu.get_barrier_semaphore()
    for k in range(1, n):
        pl.semaphore_signal(
            barrier, inc=1, device_id={"fsdp": lax.rem(me + k, n)}, device_id_type=MESH
        )
    for k in range(1, groups):
        pl.semaphore_signal(
            barrier, inc=1, device_id={"ep": lax.rem(ep + k, groups)}, device_id_type=MESH
        )

    chips = n // 2
    chip, core = me // 2, lax.rem(me, 2)
    per = 4 * own
    near = jnp.minimum(chip, chips - 1 - chip)
    forward = jnp.where(chip < chips - near - 1, 1, -1)
    both = 2 * near * per
    far = (chips - 1) * per

    def piece_of(t):
        pair = lax.rem(t, 2 * per)
        tail = t - both
        two = t < both
        away = t < far
        shift = jnp.where(
            two,
            (t // (2 * per) + 1) * (1 - 2 * lax.rem(pair, 2)),
            (near + 1 + tail // per) * forward,
        )
        piece = jnp.where(two, pair // 2, lax.rem(tail, per))
        piece = jnp.where(away, piece, t - far)
        to_chip = jnp.where(away, chip + shift, chip)
        which = lax.rem(piece, 2)
        rest = piece // 2
        on_core = jnp.where(away, which, jnp.where(piece < 2 * own, 1 - core, core))
        rest = jnp.where(away, rest, lax.rem(piece, 2 * own))
        return to_chip * 2 + on_core, lax.rem(rest, 2), rest // 2

    steps = 2 * experts
    remote = steps - 2 * own

    def load(t, act):
        device, tensor, expert = piece_of(t)
        slot = lax.rem(t, SLOTS)
        at = device * own + expert
        for k, (a, b) in enumerate(((train_gate, other_gate), (train_up, other_up))):

            @pl.when(tensor == k)
            def _():
                for source, target, sem in ((a, wide, wide_sem), (b, narrow, narrow_sem)):
                    copy = pltpu.make_async_copy(source.at[at], target.at[slot], sem.at[slot])
                    getattr(copy, act)()

    def piece_copy(t, source, sem):
        device, tensor, expert = piece_of(t)
        which = tensor * own + expert
        return pltpu.make_async_remote_copy(
            src_ref=send.at[t],
            dst_ref=landed.at[which, pl.ds(source * rows, rows), :],
            send_sem=send_sem,
            recv_sem=land_sem.at[sem, which],
            device_id={"fsdp": device},
            device_id_type=MESH,
        )

    for t in range(SLOTS - 1):
        load(t, "start")
    for k in range(2 * own):
        total[k] = jnp.zeros_like(total[k])
    pl.semaphore_wait(barrier, n - 1 + groups - 1)

    home = out_router.at[me, pl.ds(ep * band, band), :]
    pltpu.make_async_copy(router, home, row_recv).start()
    for k in range(1, n):
        pltpu.make_async_remote_copy(
            src_ref=router,
            dst_ref=home,
            send_sem=row_send,
            recv_sem=row_recv,
            device_id={"fsdp": lax.rem(me + k, n)},
            device_id_type=MESH,
        ).start()

    def fetch(t):
        @pl.when(t + SLOTS - 1 < steps)
        def _():
            load(t + SLOTS - 1, "start")

        load(t, "wait")
        return lax.rem(t, SLOTS)

    def step(t, _):
        slot = fetch(t)

        def chunk(r, _):
            at = pl.ds(pl.multiple_of(r * ROWS, ROWS), ROWS)
            latest = wide[slot, at, :] + narrow[slot, at, :].astype(jnp.float32)
            send[t, at, :] = latest.astype(jnp.bfloat16)
            return 0

        lax.fori_loop(0, rows // ROWS, chunk, 0)

        @pl.when(t > 0)
        def _():
            piece_copy(t - 1, me, me).start()

        return 0

    lax.fori_loop(0, remote, step, 0)
    piece_copy(remote - 1, me, me).start()

    def stay(t, _):
        _, tensor, expert = piece_of(t)
        which = tensor * own + expert
        slot = fetch(t)

        def chunk(r, _):
            at = pl.ds(pl.multiple_of(r * ROWS, ROWS), ROWS)
            to = pl.ds(pl.multiple_of(me * rows + r * ROWS, ROWS), ROWS)
            latest = wide[slot, at, :] + narrow[slot, at, :].astype(jnp.float32)
            landed[which, to, :] = latest.astype(jnp.bfloat16)
            return 0

        lax.fori_loop(0, rows // ROWS, chunk, 0)
        return 0

    lax.fori_loop(remote, steps, stay, 0)

    def fold(which, source):
        def chunk(r, held):
            at = pl.ds(pl.multiple_of(source * rows + r * ROWS, ROWS), ROWS)
            size = jnp.abs(landed[which, at, :].astype(jnp.float32))
            return held + jnp.sum(size.reshape(ROWS // 8, 8, width), axis=0)

        total[which] = lax.fori_loop(0, rows // ROWS, chunk, total[which])

    def fold_own(which, _):
        fold(which, me)
        return 0

    lax.fori_loop(0, 2 * own, fold_own, 0)

    columns = out_router.at[:, pl.ds(ep * band, band), :]
    pltpu.make_async_copy(columns, columns, row_recv).wait()
    for k in range(1, groups):
        pltpu.make_async_remote_copy(
            src_ref=columns,
            dst_ref=columns,
            send_sem=col_send,
            recv_sem=col_recv,
            device_id={"ep": lax.rem(ep + k, groups)},
            device_id_type=MESH,
        ).start()
    others = out_router.at[:, pl.ds(0, (groups - 1) * band), :]
    pltpu.make_async_copy(others, others, col_recv).wait()
    pltpu.make_async_copy(others, others, col_send).wait()
    sent = out_router.at[pl.ds(0, n - 1), pl.ds(0, band), :]
    pltpu.make_async_copy(sent, sent, row_send).wait()

    def take(u, _):
        t = lax.rem(u + far, remote)
        source, tensor, expert = piece_of(t)
        piece_copy(t, source, source).wait_recv()
        fold(tensor * own + expert, source)
        return 0

    lax.fori_loop(0, remote, take, 0)
    for k in range(2 * own):
        mean[pl.ds(k, 1), :] = jnp.sum(total[k], axis=0, keepdims=True) / (n * rows)

    def gone(t, _):
        piece_copy(t, me, me).wait_send()
        return 0

    lax.fori_loop(0, remote, gone, 0)


def finish(own, landed, mean, ready_gate, ready_up, scale_gate, scale_up, held, sem):
    depth = landed.shape[1]
    slots, size, _ = held.shape
    parts = depth // size
    scale_gate[...] = mean[pl.ds(0, own), :]
    scale_up[...] = mean[pl.ds(own, own), :]
    for k in range(2 * own):
        over = 1.0 / mean[pl.ds(k, 1), :]
        out = (ready_gate if k < own else ready_up).at[k % own]

        def put(c, out=out, k=k):
            slot = lax.rem(k * parts + c, slots)
            to = pl.ds(pl.multiple_of(c * size, size), size)
            return pltpu.make_async_copy(held.at[slot], out.at[to, :], sem.at[slot])

        def part(c, _, over=over, put=put, k=k):
            slot = lax.rem(k * parts + c, slots)

            @pl.when(k * parts + c >= slots)
            def _():
                put(c).wait()

            def chunk(r, _):
                at = pl.ds(pl.multiple_of(r * ROWS, ROWS), ROWS)
                of = pl.ds(pl.multiple_of(c * size + r * ROWS, ROWS), ROWS)
                value = landed[k, of, :].astype(jnp.float32) * over
                held[slot, at, :] = value.astype(jnp.bfloat16)
                return 0

            lax.fori_loop(0, size // ROWS, chunk, 0)

            @pl.when(c > 0)
            def _():
                put(c - 1).start()

            return 0

        lax.fori_loop(0, parts, part, 0)
        put(parts - 1).start()
    for slot in range(min(slots, 2 * own * parts)):
        pltpu.make_async_copy(held.at[slot], ready_up.at[0, pl.ds(0, size), :], sem.at[slot]).wait()


def shards(n, groups, train_gate, other_gate, train_up, other_up, router_weight, router_gain):
    experts, rows, width = train_gate.shape
    own = experts // n
    part_router = (router_weight * router_gain[:, None]).astype(jnp.bfloat16).T
    band, depth = part_router.shape
    anywhere = pl.BlockSpec(memory_space=pl.ANY)
    inside = pl.BlockSpec(memory_space=pltpu.VMEM)
    mean, landed, router = pl.pallas_call(
        functools.partial(exchange, n, groups),
        out_shape=(
            pltpu.VMEM((2 * own, width), jnp.float32),
            pltpu.VMEM((2 * own, n * rows, width), jnp.bfloat16),
            jax.ShapeDtypeStruct((n, groups * band, depth), jnp.bfloat16),
        ),
        in_specs=[pl.BlockSpec(memory_space=pltpu.HBM)] * 5,
        out_specs=(inside, inside, anywhere),
        scratch_shapes=[
            pltpu.VMEM((SLOTS, rows, width), jnp.float32),
            pltpu.VMEM((SLOTS, rows, width), jnp.bfloat16),
            pltpu.VMEM((2 * experts - 2 * own, rows, width), jnp.bfloat16),
            pltpu.VMEM((2 * own, 8, width), jnp.float32),
            pltpu.SemaphoreType.DMA((SLOTS,)),
            pltpu.SemaphoreType.DMA((SLOTS,)),
            pltpu.SemaphoreType.DMA((n, 2 * own)),
        ]
        + [pltpu.SemaphoreType.DMA] * 5,
        compiler_params=pltpu.CompilerParams(
            collective_id=0, has_side_effects=True, vmem_limit_bytes=34 * 2**20
        ),
    )(train_gate, other_gate, train_up, other_up, part_router)

    ready = jax.ShapeDtypeStruct((own, n * rows, width), jnp.bfloat16)
    scale = jax.ShapeDtypeStruct((own, width), jnp.float32)
    size = min(256, n * rows)
    ready_gate, ready_up, scale_gate, scale_up = pl.pallas_call(
        functools.partial(finish, own),
        out_shape=(ready, ready, scale, scale),
        in_specs=[inside, inside],
        out_specs=(anywhere, anywhere, inside, inside),
        scratch_shapes=[
            pltpu.VMEM((8, size, width), jnp.bfloat16),
            pltpu.SemaphoreType.DMA((8,)),
        ],
        compiler_params=pltpu.CompilerParams(vmem_limit_bytes=16 * 2**20),
    )(landed, mean)
    serve_router = router.transpose(0, 2, 1).reshape(n * depth, groups * band)
    return ready_gate, ready_up, scale_gate, scale_up, serve_router


def solution(mesh):
    placed = (
        P("ep", "fsdp", None),
        P("ep", "fsdp", None),
        P("ep", "fsdp", None),
        P("ep", "fsdp", None),
        P("fsdp", "ep"),
        P("fsdp"),
    )
    return jax.shard_map(
        functools.partial(shards, mesh.shape["fsdp"], mesh.shape["ep"]),
        mesh=mesh,
        in_specs=placed,
        out_specs=(
            P(("ep", "fsdp"), None, None),
            P(("ep", "fsdp"), None, None),
            P(("ep", "fsdp"), None),
            P(("ep", "fsdp"), None),
            P(),
        ),
        check_vma=False,
    )
```

time: 586 us -> 566 us (0.966)
  Pallas kernels: 577 us -> 563 us
    pallas_call x2, Pallas kernels: 577 us -> 563 us  [the longest x1 553 us: shards(): pl.pallas_call(functools.partial(exchange, n, groups), out_shape=(pltpu.V...]
where the time goes in v2:
time: 566 us
  Pallas kernels  563 us (99%)
    pallas_call x1, Pallas kernels, shards(): pl.pallas_call(functools.partial(exchange, n, groups), out_shape=(pltpu.V...  553 us

profile of v2, /device:TPU:1, one launch (start us, length us, event | category | flops | bytes accessed | tf_op | source)
XLA Modules:
  0.0 565.7 jit_solution(12598420031056088292)
XLA Ops:
  0.6 1.4 fusion.router
  2.0 553.0 %shard_map.101 = (f32[8,768]{1,0:T(8,128)S(1)}, bf16[8,2048,768]{2,1,0:T(8,128)(2,1)S(1)}, bf16[8,128,256]{2,1,0:T(8,128)(2,1)}) custom-call(f32[32,256,768]{2,1,0:T(8,128)} %train_gate.1, bf16[32,256,768]{2,1,0:T(8,128)(2,1)} %other_gate.1, f32[32,256,768]{2,1,0:T(8,128)} %train_up.1, bf16[32,256,768]{2,1,0:T(8,128)(2,1)} %other_up.1, ...), custom_call_target="tpu_custom_call" | custom-call | tf_op jit(solution)/shard_map/pallas_call | solution.py:271
  555.0 0.0 copy-start
  555.0 9.6 %shard_map.102 = (bf16[4,2048,768]{2,1,0:T(8,128)(2,1)}, bf16[4,2048,768]{2,1,0:T(8,128)(2,1)}, f32[4,768]{1,0:T(4,128)}, f32[4,768]{1,0:T(4,128)}) custom-call(bf16[8,2048,768]{2,1,0:T(8,128)(2,1)S(1)} %get-tuple-element.12.landed, f32[8,768]{1,0:T(8,128)S(1)} %get-tuple-element.13.mean), custom_call_target="tpu_custom_call" | custom-call | tf_op jit(solution)/shard_map/pallas_call | solution.py:298
  564.7 0.0 copy-done
  564.7 1.0 copy.11
Async XLA Ops:
  555.0 9.7 %copy-start = (bf16[8,128,256]{2,1,0:T(8,128)(2,1)S(1)}, bf16[8,128,256]{2,1,0:T(8,128)(2,1)}, u32[]{:S(2)}) copy-start(bf16[8,128,256]{2,1,0:T(8,128)(2,1)} %get-tuple-element.18) | copy-start | bytes 1572868

commit v3 on v2

--- a/solution.py
+++ b/solution.py
@@ -19,7 +19,8 @@
     other_gate,
     train_up,
     other_up,
-    router,
+    weight,
+    gain,
     mean,
     landed,
     out_router,
@@ -27,12 +28,19 @@
     narrow,
     send,
     total,
+    weight_in,
+    gain_in,
+    router,
+    weight_sem,
+    gain_sem,
     wide_sem,
     narrow_sem,
     land_sem,
     send_sem,
     row_send,
     row_recv,
+    swap_send,
+    swap_recv,
     col_send,
     col_recv,
 ):
@@ -40,7 +48,7 @@
     ep = lax.axis_index("ep")
     experts, rows, width = train_gate.shape
     own = experts // n
-    band = router.shape[0]
+    band = weight.shape[0]
 
     barrier = pltpu.get_barrier_semaphore()
     for k in range(1, n):
@@ -108,19 +116,26 @@
 
     for t in range(SLOTS - 1):
         load(t, "start")
+    weight_copy = pltpu.make_async_copy(weight, weight_in, weight_sem)
+    gain_copy = pltpu.make_async_copy(gain, gain_in, gain_sem)
+    weight_copy.start()
+    gain_copy.start()
     for k in range(2 * own):
         total[k] = jnp.zeros_like(total[k])
+    weight_copy.wait()
+    gain_copy.wait()
+    router[...] = (weight_in[...] * gain_in[...]).astype(jnp.bfloat16)
     pl.semaphore_wait(barrier, n - 1 + groups - 1)
 
-    home = out_router.at[me, pl.ds(ep * band, band), :]
+    home = out_router.at[chip, core, pl.ds(ep * band, band), :]
     pltpu.make_async_copy(router, home, row_recv).start()
-    for k in range(1, n):
+    for k in range(1, chips):
         pltpu.make_async_remote_copy(
             src_ref=router,
             dst_ref=home,
             send_sem=row_send,
             recv_sem=row_recv,
-            device_id={"fsdp": lax.rem(me + k, n)},
+            device_id={"fsdp": lax.rem(chip + k, chips) * 2 + core},
             device_id_type=MESH,
         ).start()
 
@@ -183,8 +198,19 @@
 
     lax.fori_loop(0, 2 * own, fold_own, 0)
 
-    columns = out_router.at[:, pl.ds(ep * band, band), :]
-    pltpu.make_async_copy(columns, columns, row_recv).wait()
+    mine = out_router.at[:, core, pl.ds(ep * band, band), :]
+    pltpu.make_async_copy(mine, mine, row_recv).wait()
+    swap = pltpu.make_async_remote_copy(
+        src_ref=mine,
+        dst_ref=mine,
+        send_sem=swap_send,
+        recv_sem=swap_recv,
+        device_id={"fsdp": chip * 2 + 1 - core},
+        device_id_type=MESH,
+    )
+    swap.start()
+    swap.wait()
+    columns = out_router.at[:, :, pl.ds(ep * band, band), :]
     for k in range(1, groups):
         pltpu.make_async_remote_copy(
             src_ref=columns,
@@ -194,10 +220,10 @@
             device_id={"ep": lax.rem(ep + k, groups)},
             device_id_type=MESH,
         ).start()
-    others = out_router.at[:, pl.ds(0, (groups - 1) * band), :]
+    others = out_router.at[:, :, pl.ds(0, (groups - 1) * band), :]
     pltpu.make_async_copy(others, others, col_recv).wait()
     pltpu.make_async_copy(others, others, col_send).wait()
-    sent = out_router.at[pl.ds(0, n - 1), pl.ds(0, band), :]
+    sent = out_router.at[pl.ds(0, chips - 1), 0, pl.ds(0, band), :]
     pltpu.make_async_copy(sent, sent, row_send).wait()
 
     def take(u, _):
@@ -211,14 +237,20 @@
     for k in range(2 * own):
         mean[pl.ds(k, 1), :] = jnp.sum(total[k], axis=0, keepdims=True) / (n * rows)
 
-    def gone(t, _):
-        piece_copy(t, me, me).wait_send()
-        return 0
-
-    lax.fori_loop(0, remote, gone, 0)
-
-
-def finish(own, landed, mean, ready_gate, ready_up, scale_gate, scale_up, held, sem):
+    pltpu.make_async_copy(send, send, send_sem).wait()
+
+
+def finish(
+    own,
+    landed,
+    mean,
+    ready_gate,
+    ready_up,
+    scale_gate,
+    scale_up,
+    held,
+    sem,
+):
     depth = landed.shape[1]
     slots, size, _ = held.shape
     parts = depth // size
@@ -264,40 +296,50 @@
 def shards(n, groups, train_gate, other_gate, train_up, other_up, router_weight, router_gain):
     experts, rows, width = train_gate.shape
     own = experts // n
-    part_router = (router_weight * router_gain[:, None]).astype(jnp.bfloat16).T
-    band, depth = part_router.shape
+    depth, band = router_weight.shape
     anywhere = pl.BlockSpec(memory_space=pl.ANY)
+    outside = pl.BlockSpec(memory_space=pltpu.HBM)
     inside = pl.BlockSpec(memory_space=pltpu.VMEM)
     mean, landed, router = pl.pallas_call(
         functools.partial(exchange, n, groups),
         out_shape=(
             pltpu.VMEM((2 * own, width), jnp.float32),
             pltpu.VMEM((2 * own, n * rows, width), jnp.bfloat16),
-            jax.ShapeDtypeStruct((n, groups * band, depth), jnp.bfloat16),
+            pltpu.HBM((n // 2, 2, groups * band, depth), jnp.bfloat16),
         ),
-        in_specs=[pl.BlockSpec(memory_space=pltpu.HBM)] * 5,
-        out_specs=(inside, inside, anywhere),
+        in_specs=[outside] * 6,
+        out_specs=(inside, inside, outside),
         scratch_shapes=[
             pltpu.VMEM((SLOTS, rows, width), jnp.float32),
             pltpu.VMEM((SLOTS, rows, width), jnp.bfloat16),
             pltpu.VMEM((2 * experts - 2 * own, rows, width), jnp.bfloat16),
             pltpu.VMEM((2 * own, 8, width), jnp.float32),
+            pltpu.VMEM((band, depth), jnp.float32),
+            pltpu.VMEM((1, depth), jnp.float32),
+            pltpu.VMEM((band, depth), jnp.bfloat16),
+            pltpu.SemaphoreType.DMA,
+            pltpu.SemaphoreType.DMA,
             pltpu.SemaphoreType.DMA((SLOTS,)),
             pltpu.SemaphoreType.DMA((SLOTS,)),
             pltpu.SemaphoreType.DMA((n, 2 * own)),
         ]
-        + [pltpu.SemaphoreType.DMA] * 5,
+        + [pltpu.SemaphoreType.DMA] * 7,
         compiler_params=pltpu.CompilerParams(
             collective_id=0, has_side_effects=True, vmem_limit_bytes=34 * 2**20
         ),
-    )(train_gate, other_gate, train_up, other_up, part_router)
+    )(train_gate, other_gate, train_up, other_up, router_weight.T, router_gain[None])
 
     ready = jax.ShapeDtypeStruct((own, n * rows, width), jnp.bfloat16)
     scale = jax.ShapeDtypeStruct((own, width), jnp.float32)
     size = min(256, n * rows)
     ready_gate, ready_up, scale_gate, scale_up = pl.pallas_call(
         functools.partial(finish, own),
-        out_shape=(ready, ready, scale, scale),
+        out_shape=(
+            ready,
+            ready,
+            scale,
+            scale,
+        ),
         in_specs=[inside, inside],
         out_specs=(anywhere, anywhere, inside, inside),
         scratch_shapes=[
@@ -306,7 +348,7 @@
         ],
         compiler_params=pltpu.CompilerParams(vmem_limit_bytes=16 * 2**20),
     )(landed, mean)
-    serve_router = router.transpose(0, 2, 1).reshape(n * depth, groups * band)
+    serve_router = router.transpose(0, 1, 3, 2).reshape(n * depth, groups * band)
     return ready_gate, ready_up, scale_gate, scale_up, serve_router
 
 

time: 566 us -> 563 us (level)
  no operation moved by 1% of the time
where the time goes in v3:
time: 563 us
  Pallas kernels  561 us (100%)
    pallas_call x1, Pallas kernels, shards(): pl.pallas_call(functools.partial(exchange, n, groups), out_shape=(pltpu.V...  551 us

profile of v3, /device:TPU:1, one launch (start us, length us, event | category | flops | bytes accessed | tf_op | source)
XLA Modules:
  0.0 562.7 jit_solution(919125020551165010)
XLA Ops:
  0.6 551.4 %shard_map.101 = (f32[8,768]{1,0:T(8,128)S(1)}, bf16[8,2048,768]{2,1,0:T(8,128)(2,1)S(1)}, bf16[4,2,128,256]{3,2,1,0:T(8,128)(2,1)}) custom-call(f32[32,256,768]{2,1,0:T(8,128)} %train_gate.1, bf16[32,256,768]{2,1,0:T(8,128)(2,1)} %other_gate.1, f32[32,256,768]{2,1,0:T(8,128)} %train_up.1, bf16[32,256,768]{2,1,0:T(8,128)(2,1)} %other_up.1, ...), custom_call_target="tpu_custom_call" | custom-call | tf_op jit(solution)/shard_map/pallas_call | solution.py:303
  552.0 0.0 copy-start
  552.0 9.6 %shard_map.102 = (bf16[4,2048,768]{2,1,0:T(8,128)(2,1)}, bf16[4,2048,768]{2,1,0:T(8,128)(2,1)}, f32[4,768]{1,0:T(4,128)}, f32[4,768]{1,0:T(4,128)}) custom-call(bf16[8,2048,768]{2,1,0:T(8,128)(2,1)S(1)} %get-tuple-element.12.landed, f32[8,768]{1,0:T(8,128)S(1)} %get-tuple-element.13.mean), custom_call_target="tpu_custom_call" | custom-call | tf_op jit(solution)/shard_map/pallas_call | solution.py:335
  561.6 0.0 copy-done
  561.7 1.0 copy.11
Async XLA Ops:
  552.0 9.7 %copy-start = (bf16[4,2,128,256]{3,2,1,0:T(8,128)(2,1)S(1)}, bf16[4,2,128,256]{3,2,1,0:T(8,128)(2,1)}, u32[]{:S(2)}) copy-start(bf16[4,2,128,256]{3,2,1,0:T(8,128)(2,1)} %get-tuple-element.18) | copy-start | bytes 1572868
